TPU v7x, 32 devices: a whole 2x2x4 slice. The times are simulated.
32 devices in a mesh: owner: 4 (over x, core), rows: 8 (over z, y).
Axes of the slice: x: 2, y: 2, z: 4, core: 2. Of those that a mesh axis runs over, the one named last changes fastest.
Arguments:
- w_down: float32 [16, 6400, 4096], P('owner', None, 'rows'), may hold values from -0.109375 to 0.109375
- avg_down: bfloat16 [16, 6400, 4096], P('owner', None, 'rows'), may hold values from -0.0390625 to 0.0390625
- router_weight: float32 [4096, 16], P('rows', 'owner'), may hold values from -0.09375 to 0.09375
- router_gain: float32 [4096], P('rows'), may hold values from 0.25 to 1.75
Outputs:
- serve_down: bfloat16 [16, 6400, 4096], P('owner', 'rows')
- scale_down: float32 [16, 6400], P('owner', 'rows')
- serve_router: bfloat16 [4096, 16], replicated
All inputs are finite; a program needn't handle non-finite values. Where the computation divides by a largest or mean magnitude, that divisor is 1e-20 or more.
Results may differ from a plain program's by a relative error of at most 0.001.
Values may be sent and summed in bfloat16 or wider, within the bound.
A program may use at most 256 MiB of HBM per device.

v0:
```python
import jax
import jax.numpy as jnp
from jax import lax
from jax.sharding import PartitionSpec as P

D_MODEL = 4096


def per_device(w_down, avg_down, router_weight, router_gain):
    fresh_down = w_down + avg_down.astype(jnp.float32)
    total_down = lax.psum(jnp.sum(jnp.abs(fresh_down), axis=2), "rows")
    scale_down = total_down / D_MODEL
    narrow_down = (fresh_down / jnp.expand_dims(scale_down, 2)).astype(jnp.bfloat16)
    serve_down = lax.all_to_all(narrow_down, "rows", split_axis=1, concat_axis=2, tiled=True)
    scale_down = lax.dynamic_slice_in_dim(
        scale_down, lax.axis_index("rows") * serve_down.shape[1], serve_down.shape[1], axis=1
    )
    part_router = (router_weight * router_gain[:, None]).astype(jnp.bfloat16)
    row_router = lax.all_gather(part_router, "rows", axis=0, tiled=True)
    serve_router = lax.all_gather(row_router, "owner", axis=1, tiled=True)
    return (serve_down, scale_down, serve_router)


def solution(mesh):
    return jax.shard_map(
        per_device,
        mesh=mesh,
        in_specs=(
            P("owner", None, "rows"),
            P("owner", None, "rows"),
            P("rows", "owner"),
            P("rows"),
        ),
        out_specs=(P("owner", "rows", None), P("owner", "rows"), P()),
        check_vma=False,
    )
```

profile of v0, /device:TPU:0, one launch (start us, length us, event | category | flops | bytes accessed | tf_op | source)
XLA Modules:
  0.0 904.8 jit_solution(12173530837485246061)
XLA Ops:
  7.2 0.0 all-reduce.2.cloned.1.call-start
  7.2 24.2 %abs_reduce_fusion = f32[4,6400]{1,0:T(4,128)S(1)} fusion(f32[4,6400,512]{2,1,0:T(8,128)} %param.4, bf16[4,6400,512]{2,1,0:T(8,128)(2,1)} %param.5), kind=kLoop, calls=%fused_computation.1 | loop fusion | flops 52403200 | bytes 78745600 | tf_op jit(solution)/shard_map/reduce_sum | solution.py:11
  31.4 2.3 copy.21
  33.7 0.0 all-reduce.2.cloned.1.call-update
  33.7 135.4 %all-reduce.2.cloned.1.call-done = f32[4,6400]{0,1:T(8,128)} async-done(((f32[4,6400]{0,1:T(8,128)}), f32[4,6400]{0,1:T(8,128)}) %all-reduce.2.cloned.1.call-update) | async-done | bytes 102416 | tf_op jit(solution)/shard_map/psum | solution.py:11
  169.1 2.1 broadcast_multiply_fusion
  171.3 1.2 copy.17
  172.5 34.3 %divide_convert_fusion = bf16[4,6400,512]{2,1,0:T(8,128)(2,1)} fusion(f32[4,6400,512]{2,1,0:T(8,128)} %param.4, bf16[4,6400,512]{2,1,0:T(8,128)(2,1)} %param.5, f32[4,6400]{1,0:T(4,128)S(1)} %copy.17), kind=kLoop, calls=%fused_computation | loop fusion | flops 52428800 | bytes 104960000 | tf_op jit(solution)/shard_map/convert_element_type | solution.py:13
  206.8 33.4 %copy.18 = bf16[4,6400,512]{2,0,1:T(4,128)(2,1)} copy(bf16[4,6400,512]{2,1,0:T(8,128)(2,1)} %divide_convert_fusion) | data formatting | bytes 52428800 | tf_op jit(solution)/shard_map/convert_element_type | solution.py:13
  240.2 0.0 copy-start
  240.2 0.0 copy-start.1
  240.2 6.6 all-to-all-start
  246.8 0.0 copy-done
  246.9 0.0 copy-done.1
  246.9 585.0 %all_gather.6 = bf16[4096,4]{0,1:T(4,128)(2,1)S(1)} all-gather(bf16[512,4]{0,1:T(4,128)(2,1)S(1)} %multiply_convert_fusion), channel_id=1, replica_groups=mesh['owner'=4,'rows'=8] {'rows'}, dimensions={0}, use_global_device_ids=true | all-gather | bytes 36864 | tf_op jit(solution)/shard_map/all_gather | solution.py:19
  831.9 5.4 all-gather
  837.3 0.7 reshape.9
  838.0 0.8 constant_dynamic-slice_fusion
  838.8 1.8 copy.20
  840.6 0.0 all-to-all-done
  840.6 18.2 %copy.19 = bf16[4,800,8,512]{3,2,1,0:T(8,128)(2,1)} copy(bf16[4,800,8,512]{3,0,1,2:T(4,128)(2,1)} %bitcast.1) | data formatting | bytes 52428800 | tf_op jit(solution)/shard_map/all_to_all | solution.py:14
  858.8 39.2 %all_to_all.16 = bf16[4,800,4096]{2,1,0:T(8,128)(2,1)} reshape(bf16[4,800,8,512]{3,2,1,0:T(8,128)(2,1)} %copy.19) | data formatting | bytes 52428800 | tf_op jit(solution)/shard_map/all_to_all | solution.py:14
  (1 shorter events, 0.0 us)
Async XLA Ops:
  7.2 162.0 %all-reduce.2.cloned.1.call-start = ((), (), s32[]{:S(2)}) async-start(), calls=%async_computation.1 | async-start | bytes 6553600 | tf_op jit(solution)/shard_map/psum | solution.py:11
  240.2 6.7 copy-start
  240.2 6.7 copy-start.1
  240.2 600.4 %all-to-all-start = ((bf16[4,6400,512]{2,0,1:T(4,128)(2,1)}), bf16[4,6400,512]{2,0,1:T(4,128)(2,1)}, u32[]{:S(2)}, u32[]{:S(2)}) async-start(bf16[4,6400,512]{2,0,1:T(4,128)(2,1)} %copy.18), calls=%async_computation | async-start | bytes 52428800 | tf_op jit(solution)/shard_map/all_to_all | solution.py:14
Sparse Core Ops, SparseCore 0:
  33.9 135.2 all-reduce.1
where the time goes:
time: 906 us; the launch traced here: 905 us
  blocking collectives  590 us (65%)
  waiting for transfers between devices  135 us (15%)
  local copies, waits for them, and re-layouts  97.5 us (11%)
  other arithmetic  60.7 us (7%)
  between operations  14.1 us (2%)
    all_gather x1, blocking collectives, per_device(): row_router = lax.all_gather(part_router, 'rows', axis=0, tiled=True)  585 us
    psum x1, waiting for transfers between devices, per_device(): total_down = lax.psum(jnp.sum(jnp.abs(fresh_down), axis=2), 'rows')  135 us
    all_to_all x2, local copies, waits for them, and re-layouts, per_device(): lax.all_to_all(narrow_down, 'rows', split_axis=1, concat_axis=2, tiled=True)  57.4 us
    convert_element_type x1, other arithmetic, per_device(): (fresh_down / jnp.expand_dims(scale_down, 2)).astype(jnp.bfloat16)  34.3 us
    convert_element_type x1, local copies, waits for them, and re-layouts, per_device(): (fresh_down / jnp.expand_dims(scale_down, 2)).astype(jnp.bfloat16)  33.4 us
    reduce_sum x1, other arithmetic, per_device(): total_down = lax.psum(jnp.sum(jnp.abs(fresh_down), axis=2), 'rows')  24.2 us
  transfers between devices with their start and end apart: 2, of which 1 were waited for; matrix products, arithmetic and copies ran while one was open for 0% of the time, Pallas kernels for 0%

commit v1 on v0

--- a/solution.py
+++ b/solution.py
@@ -17,7 +17,7 @@
     )
     part_router = (router_weight * router_gain[:, None]).astype(jnp.bfloat16)
     row_router = lax.all_gather(part_router, "rows", axis=0, tiled=True)
-    serve_router = lax.all_gather(row_router, "owner", axis=1, tiled=True)
+    serve_router = jnp.concatenate(lax.all_gather(row_router, "owner"), axis=1)
     return (serve_down, scale_down, serve_router)
 
 

time: 906 us -> 906 us (level)
  no operation moved by 1% of the time
where the time goes in v1:
time: 906 us; the launch traced here: 905 us
  blocking collectives  590 us (65%)
  waiting for transfers between devices  135 us (15%)
  local copies, waits for them, and re-layouts  97.5 us (11%)
  other arithmetic  60.7 us (7%)
  between operations  14.1 us (2%)
    all_gather x1, blocking collectives, per_device(): row_router = lax.all_gather(part_router, 'rows', axis=0, tiled=True)  585 us
    psum x1, waiting for transfers between devices, per_device(): total_down = lax.psum(jnp.sum(jnp.abs(fresh_down), axis=2), 'rows')  135 us
    all_to_all x2, local copies, waits for them, and re-layouts, per_device(): lax.all_to_all(narrow_down, 'rows', split_axis=1, concat_axis=2, tiled=True)  57.4 us
    convert_element_type x1, other arithmetic, per_device(): (fresh_down / jnp.expand_dims(scale_down, 2)).astype(jnp.bfloat16)  34.3 us
    convert_element_type x1, local copies, waits for them, and re-layouts, per_device(): (fresh_down / jnp.expand_dims(scale_down, 2)).astype(jnp.bfloat16)  33.4 us
    reduce_sum x1, other arithmetic, per_device(): total_down = lax.psum(jnp.sum(jnp.abs(fresh_down), axis=2), 'rows')  24.2 us
  transfers between devices with their start and end apart: 2, of which 1 were waited for; matrix products, arithmetic and copies ran while one was open for 0% of the time, Pallas kernels for 0%

profile of v1, /device:TPU:0, one launch (start us, length us, event | category | flops | bytes accessed | tf_op | source)
XLA Modules:
  0.0 904.8 jit_solution(7164546433078577317)
XLA Ops:
  7.2 0.0 all-reduce.2.cloned.1.call-start
  7.2 24.2 %abs_reduce_fusion = f32[4,6400]{1,0:T(4,128)S(1)} fusion(f32[4,6400,512]{2,1,0:T(8,128)} %param.4, bf16[4,6400,512]{2,1,0:T(8,128)(2,1)} %param.5), kind=kLoop, calls=%fused_computation.1 | loop fusion | flops 52403200 | bytes 78745600 | tf_op jit(solution)/shard_map/reduce_sum | solution.py:11
  31.4 2.3 copy.25
  33.7 0.0 all-reduce.2.cloned.1.call-update
  33.7 135.4 %all-reduce.2.cloned.1.call-done = f32[4,6400]{0,1:T(8,128)} async-done(((f32[4,6400]{0,1:T(8,128)}), f32[4,6400]{0,1:T(8,128)}) %all-reduce.2.cloned.1.call-update) | async-done | bytes 102416 | tf_op jit(solution)/shard_map/psum | solution.py:11
  169.1 2.1 broadcast_multiply_fusion
  171.3 1.2 copy.20
  172.5 34.3 %divide_convert_fusion = bf16[4,6400,512]{2,1,0:T(8,128)(2,1)} fusion(f32[4,6400,512]{2,1,0:T(8,128)} %param.4, bf16[4,6400,512]{2,1,0:T(8,128)(2,1)} %param.5, f32[4,6400]{1,0:T(4,128)S(1)} %copy.20), kind=kLoop, calls=%fused_computation | loop fusion | flops 52428800 | bytes 104960000 | tf_op jit(solution)/shard_map/convert_element_type | solution.py:13
  206.8 33.4 %copy.21 = bf16[4,6400,512]{2,0,1:T(4,128)(2,1)} copy(bf16[4,6400,512]{2,1,0:T(8,128)(2,1)} %divide_convert_fusion) | data formatting | bytes 52428800 | tf_op jit(solution)/shard_map/convert_element_type | solution.py:13
  240.2 0.0 copy-start
  240.2 0.0 copy-start.1
  240.2 6.6 all-to-all-start
  246.8 0.0 copy-done
  246.9 0.0 copy-done.1
  246.9 585.0 %all_gather.9 = bf16[4096,4]{0,1:T(4,128)(2,1)S(1)} all-gather(bf16[512,4]{0,1:T(4,128)(2,1)S(1)} %multiply_convert_fusion), channel_id=1, replica_groups=mesh['owner'=4,'rows'=8] {'rows'}, dimensions={0}, use_global_device_ids=true | all-gather | bytes 36864 | tf_op jit(solution)/shard_map/all_gather | solution.py:19
  831.9 5.4 all-gather
  837.3 0.7 reshape.15
  838.0 0.8 constant_dynamic-slice_fusion
  838.8 1.8 copy.24
  840.6 0.0 all-to-all-done
  840.6 18.2 %copy.22 = bf16[4,800,8,512]{3,2,1,0:T(8,128)(2,1)} copy(bf16[4,800,8,512]{3,0,1,2:T(4,128)(2,1)} %bitcast.1) | data formatting | bytes 52428800 | tf_op jit(solution)/shard_map/all_to_all | solution.py:14
  858.8 39.2 %all_to_all.16 = bf16[4,800,4096]{2,1,0:T(8,128)(2,1)} reshape(bf16[4,800,8,512]{3,2,1,0:T(8,128)(2,1)} %copy.22) | data formatting | bytes 52428800 | tf_op jit(solution)/shard_map/all_to_all | solution.py:14
  (1 shorter events, 0.0 us)
Async XLA Ops:
  7.2 162.0 %all-reduce.2.cloned.1.call-start = ((), (), s32[]{:S(2)}) async-start(), calls=%async_computation.1 | async-start | bytes 6553600 | tf_op jit(solution)/shard_map/psum | solution.py:11
  240.2 6.7 copy-start
  240.2 6.7 copy-start.1
  240.2 600.4 %all-to-all-start = ((bf16[4,6400,512]{2,0,1:T(4,128)(2,1)}), bf16[4,6400,512]{2,0,1:T(4,128)(2,1)}, u32[]{:S(2)}, u32[]{:S(2)}) async-start(bf16[4,6400,512]{2,0,1:T(4,128)(2,1)} %copy.21), calls=%async_computation | async-start | bytes 52428800 | tf_op jit(solution)/shard_map/all_to_all | solution.py:14
Sparse Core Ops, SparseCore 0:
  33.9 135.2 all-reduce.1

commit v2 on v0

--- a/solution.py
+++ b/solution.py
@@ -8,7 +8,7 @@
 
 def per_device(w_down, avg_down, router_weight, router_gain):
     fresh_down = w_down + avg_down.astype(jnp.float32)
-    total_down = lax.psum(jnp.sum(jnp.abs(fresh_down), axis=2), "rows")
+    total_down = jnp.sum(lax.all_gather(jnp.sum(jnp.abs(fresh_down), axis=2), "rows"), axis=0)
     scale_down = total_down / D_MODEL
     narrow_down = (fresh_down / jnp.expand_dims(scale_down, 2)).astype(jnp.bfloat16)
     serve_down = lax.all_to_all(narrow_down, "rows", split_axis=1, concat_axis=2, tiled=True)

time: 906 us -> 781 us (0.86)
  waiting for transfers between devices: 135 us -> 0.01 us
  blocking collectives: 590 us -> 620 us
  between operations: 14.1 us -> 0.71 us
    psum x1 -> x0, waiting for transfers between devices: 135 us -> none  [per_device(): total_down = lax.psum(jnp.sum(jnp.abs(fresh_down), axis=2), 'rows')]
    all_gather x0 -> x1, blocking collectives: none -> 33.9 us  [per_device(): lax.all_gather(jnp.sum(jnp.abs(fresh_down), axis=2), 'rows')]
    reduce_sum x1 -> x2, other arithmetic: 24.2 us -> 24.4 us  [the longest x1 24.2 us: per_device(): jnp.sum(jnp.abs(fresh_down), axis=2)]
  transfers between devices with their start and end apart: 2 -> 1, of which waited for: 1 -> 0; matrix products, arithmetic and copies ran while one was open for 0% -> 0% of each run, Pallas kernels for 0% -> 0%
where the time goes in v2:
time: 781 us; the launch traced here: 780 us
  blocking collectives  620 us (79%)
  local copies, waits for them, and re-layouts  94.5 us (12%)
  other arithmetic  58.7 us (8%)
    all_gather x1, blocking collectives, per_device(): row_router = lax.all_gather(part_router, 'rows', axis=0, tiled=True)  580 us
    all_to_all x2, local copies, waits for them, and re-layouts, per_device(): lax.all_to_all(narrow_down, 'rows', split_axis=1, concat_axis=2, tiled=True)  57.4 us
    convert_element_type x1, other arithmetic, per_device(): (fresh_down / jnp.expand_dims(scale_down, 2)).astype(jnp.bfloat16)  34.3 us
    all_gather x1, blocking collectives, per_device(): lax.all_gather(jnp.sum(jnp.abs(fresh_down), axis=2), 'rows')  33.9 us
    convert_element_type x1, local copies, waits for them, and re-layouts, per_device(): (fresh_down / jnp.expand_dims(scale_down, 2)).astype(jnp.bfloat16)  33.4 us
    reduce_sum x1, other arithmetic, per_device(): jnp.sum(jnp.abs(fresh_down), axis=2)  24.2 us
  transfers between devices with their start and end apart: 1, of which 0 were waited for; matrix products, arithmetic and copies ran while one was open for 0% of the time, Pallas kernels for 0%

profile of v2, /device:TPU:0, one launch (start us, length us, event | category | flops | bytes accessed | tf_op | source)
XLA Modules:
  0.0 780.0 jit_solution(4935870876903753817)
XLA Ops:
  0.6 24.2 %abs_reduce_fusion = f32[4,6400]{1,0:T(4,128)S(1)} fusion(f32[4,6400,512]{2,1,0:T(8,128)} %param.4, bf16[4,6400,512]{2,1,0:T(8,128)(2,1)} %param.5), kind=kLoop, calls=%fused_computation.1 | loop fusion | flops 52403200 | bytes 78745600 | tf_op jit(solution)/shard_map/reduce_sum | solution.py:11
  24.9 1.1 copy.21
  26.0 1.2 copy.18
  27.2 33.9 %all-gather.1 = f32[8,4,6400]{2,1,0:T(4,128)S(1)} all-gather(f32[1,4,6400]{2,1,0:T(4,128)S(1)} %copy.18), channel_id=2, replica_groups=mesh['owner'=4,'rows'=8] {'rows'}, dimensions={0}, use_global_device_ids=true | all-gather | bytes 921600 | tf_op jit(solution)/shard_map/all_gather | solution.py:11
  61.2 0.1 reduce_sum.19
  61.3 34.3 %divide_convert_fusion = bf16[4,6400,512]{2,1,0:T(8,128)(2,1)} fusion(f32[4,6400,512]{2,1,0:T(8,128)} %param.4, bf16[4,6400,512]{2,1,0:T(8,128)(2,1)} %param.5, f32[4,6400]{1,0:T(4,128)S(1)} %broadcast_multiply_fusion), kind=kLoop, calls=%fused_computation | loop fusion | flops 52428800 | bytes 104960000 | tf_op jit(solution)/shard_map/convert_element_type | solution.py:13
  95.6 0.0 copy-start
  95.6 0.0 copy-start.1
  95.6 33.4 %copy.19 = bf16[4,6400,512]{2,0,1:T(4,128)(2,1)} copy(bf16[4,6400,512]{2,1,0:T(8,128)(2,1)} %divide_convert_fusion) | data formatting | bytes 52428800 | tf_op jit(solution)/shard_map/convert_element_type | solution.py:13
  129.0 6.5 all-to-all-start
  135.5 0.0 copy-done
  135.5 0.0 copy-done.1
  135.6 580.3 %all_gather.14 = bf16[4096,4]{0,1:T(4,128)(2,1)S(1)} all-gather(bf16[512,4]{0,1:T(4,128)(2,1)S(1)} %multiply_convert_fusion), channel_id=1, replica_groups=mesh['owner'=4,'rows'=8] {'rows'}, dimensions={0}, use_global_device_ids=true | all-gather | bytes 36864 | tf_op jit(solution)/shard_map/all_gather | solution.py:19
  715.8 5.4 all-gather.2
  721.2 0.7 reshape.14
  721.9 0.7 constant_dynamic-slice_fusion
  722.6 0.0 all-to-all-done
  722.6 18.2 %copy.20 = bf16[4,800,8,512]{3,2,1,0:T(8,128)(2,1)} copy(bf16[4,800,8,512]{3,0,1,2:T(4,128)(2,1)} %bitcast.2) | data formatting | bytes 52428800 | tf_op jit(solution)/shard_map/all_to_all | solution.py:14
  740.8 39.2 %all_to_all.16 = bf16[4,800,4096]{2,1,0:T(8,128)(2,1)} reshape(bf16[4,800,8,512]{3,2,1,0:T(8,128)(2,1)} %copy.20) | data formatting | bytes 52428800 | tf_op jit(solution)/shard_map/all_to_all | solution.py:14
  (2 shorter events, 0.0 us)
Async XLA Ops:
  95.6 39.9 %copy-start = (f32[512,4]{0,1:T(4,128)S(1)}, f32[512,4]{0,1:T(4,128)}, u32[]{:S(2)}) copy-start(f32[512,4]{0,1:T(4,128)} %param.6) | copy-start | bytes 24580
  95.6 39.9 %copy-start.1 = (f32[512]{0:T(512)S(1)}, f32[512]{0:T(512)}, u32[]{:S(2)}) copy-start(f32[512]{0:T(512)} %param.7) | copy-start | bytes 6148
  129.0 593.6 %all-to-all-start = ((bf16[4,6400,512]{2,0,1:T(4,128)(2,1)}), bf16[4,6400,512]{2,0,1:T(4,128)(2,1)}, u32[]{:S(2)}, u32[]{:S(2)}) async-start(bf16[4,6400,512]{2,0,1:T(4,128)(2,1)} %copy.19), calls=%async_computation | async-start | bytes 52428800 | tf_op jit(solution)/shard_map/all_to_all | solution.py:14

commit v3 on v0

--- a/solution.py
+++ b/solution.py
@@ -11,7 +11,12 @@
     total_down = lax.psum(jnp.sum(jnp.abs(fresh_down), axis=2), "rows")
     scale_down = total_down / D_MODEL
     narrow_down = (fresh_down / jnp.expand_dims(scale_down, 2)).astype(jnp.bfloat16)
-    serve_down = lax.all_to_all(narrow_down, "rows", split_axis=1, concat_axis=2, tiled=True)
+    serve_down = jnp.concatenate(
+        lax.all_to_all(
+            jnp.stack(jnp.split(narrow_down, lax.axis_size("rows"), axis=1)), "rows", 0, 0
+        ),
+        axis=2,
+    )
     scale_down = lax.dynamic_slice_in_dim(
         scale_down, lax.axis_index("rows") * serve_down.shape[1], serve_down.shape[1], axis=1
     )

time: 906 us -> 792 us (0.87)
  waiting for transfers between devices: 135 us -> 72.4 us
  local copies, waits for them, and re-layouts: 97.5 us -> 49.9 us
    psum x1, waiting for transfers between devices: 135 us -> 72.4 us  [per_device(): total_down = lax.psum(jnp.sum(jnp.abs(fresh_down), axis=2), 'rows')]
    all_to_all x2 -> x0, local copies, waits for them, and re-layouts: 57.4 us -> none  [per_device(): lax.all_to_all(narrow_down, 'rows', split_axis=1, concat_axis=2, tiled=True)]
    convert_element_type x1 -> x0, local copies, waits for them, and re-layouts: 33.4 us -> none  [per_device(): (fresh_down / jnp.expand_dims(scale_down, 2)).astype(jnp.bfloat16)]
    unnamed x7 -> x12, local copies, waits for them, and re-layouts: 4.74 us -> 27.5 us
    reshape x0 -> x1, local copies, waits for them, and re-layouts: none -> 17.9 us  [per_device(): jnp.concatenate(lax.all_to_all(jnp.stack(jnp.split(narrow_down, lax.axis_...]
where the time goes in v3:
time: 792 us
  blocking collectives  589 us (74%)
  waiting for transfers between devices  72.4 us (9%)
  other arithmetic  60.1 us (8%)
  local copies, waits for them, and re-layouts  49.9 us (6%)
  between operations  14.1 us (2%)
    all_gather x1, blocking collectives, per_device(): row_router = lax.all_gather(part_router, 'rows', axis=0, tiled=True)  583 us
    psum x1, waiting for transfers between devices, per_device(): total_down = lax.psum(jnp.sum(jnp.abs(fresh_down), axis=2), 'rows')  72.4 us
    convert_element_type x1, other arithmetic, per_device(): (fresh_down / jnp.expand_dims(scale_down, 2)).astype(jnp.bfloat16)  34.3 us
    unnamed x12, local copies, waits for them, and re-layouts  27.5 us
    reduce_sum x1, other arithmetic, per_device(): total_down = lax.psum(jnp.sum(jnp.abs(fresh_down), axis=2), 'rows')  24.9 us
    reshape x1, local copies, waits for them, and re-layouts, per_device(): jnp.concatenate(lax.all_to_all(jnp.stack(jnp.split(narrow_down, lax.axis_...  17.9 us
  transfers between devices with their start and end apart: 2, of which 1 were waited for; matrix products, arithmetic and copies ran while one was open for 0% of the time, Pallas kernels for 0%

profile of v3, /device:TPU:0, one launch (start us, length us, event | category | flops | bytes accessed | tf_op | source)
XLA Modules:
  0.0 791.9 jit_solution(5396997361598960320)
XLA Ops:
  7.2 0.0 all-reduce.2.cloned.1.call-start
  7.2 24.9 %abs_reduce_fusion = f32[4,6400]{1,0:T(4,128)} fusion(f32[4,6400,512]{2,1,0:T(8,128)} %param.4, bf16[4,6400,512]{2,1,0:T(8,128)(2,1)} %param.5), kind=kLoop, calls=%fused_computation.1 | loop fusion | flops 52403200 | bytes 78745600 | tf_op jit(solution)/shard_map/reduce_sum | solution.py:11
  32.1 0.0 all-reduce.2.cloned.1.call-update
  32.1 72.4 %all-reduce.2.cloned.1.call-done = f32[4,6400]{1,0:T(4,128)} async-done(((f32[4,6400]{1,0:T(4,128)}), f32[4,6400]{1,0:T(4,128)}) %all-reduce.2.cloned.1.call-update) | async-done | bytes 102416 | tf_op jit(solution)/shard_map/psum | solution.py:11
  104.5 0.9 broadcast_multiply_fusion
  105.4 34.3 %divide_convert_fusion = bf16[4,6400,512]{2,1,0:T(8,128)(2,1)} fusion(f32[4,6400,512]{2,1,0:T(8,128)} %param.4, bf16[4,6400,512]{2,1,0:T(8,128)(2,1)} %param.5, f32[4,6400]{1,0:T(4,128)S(1)} %broadcast_multiply_fusion), kind=kLoop, calls=%fused_computation | loop fusion | flops 52428800 | bytes 104960000 | tf_op jit(solution)/shard_map/convert_element_type | solution.py:13
  139.7 3.8 fusion.7
  143.5 3.8 fusion.6
  147.4 3.8 fusion.5
  151.2 3.8 fusion.4
  155.0 3.9 fusion.3
  158.9 3.8 fusion.2
  162.7 3.8 fusion.1
  166.5 3.8 fusion
  170.3 0.0 copy-start
  170.3 0.0 copy-start.1
  170.3 6.6 all-to-all-start
  177.0 0.0 copy-done
  177.0 0.0 copy-done.1
  177.0 583.4 %all_gather.6 = bf16[4096,4]{0,1:T(4,128)(2,1)S(1)} all-gather(bf16[512,4]{0,1:T(4,128)(2,1)S(1)} %multiply_convert_fusion), channel_id=1, replica_groups=mesh['owner'=4,'rows'=8] {'rows'}, dimensions={0}, use_global_device_ids=true | all-gather | bytes 36864 | tf_op jit(solution)/shard_map/all_gather | solution.py:24
  760.4 5.4 all-gather
  765.8 0.7 reshape.17
  766.5 0.7 constant_dynamic-slice_fusion
  767.2 0.0 all-to-all-done
  767.2 17.9 %copy.9 = bf16[8,4,100,8,512]{4,3,0,2,1:T(8,128)(2,1)} copy(bf16[8,4,100,8,512]{4,3,2,1,0:T(8,128)(2,1)} %bitcast.13) | data formatting | bytes 52428800 | tf_op jit(solution)/shard_map/reshape | solution.py:14
  (1 shorter events, 0.0 us)
Async XLA Ops:
  7.2 97.3 %all-reduce.2.cloned.1.call-start = ((), (), s32[]{:S(2)}) async-start(), calls=%async_computation.1 | async-start | bytes 204800 | tf_op jit(solution)/shard_map/psum | solution.py:11
  170.3 6.6 copy-start
  170.3 6.6 copy-start.1
  170.3 596.9 %all-to-all-start = ((bf16[8,4,800,512]{3,2,1,0:T(8,128)(2,1)}), bf16[8,4,800,512]{3,2,1,0:T(8,128)(2,1)}, u32[]{:S(2)}, u32[]{:S(2)}) async-start(bf16[8,4,800,512]{3,2,1,0:T(8,128)(2,1)} %fusion), calls=%async_computation | async-start | bytes 52428800 | tf_op jit(solution)/shard_map/all_to_all | solution.py:15
Sparse Core Ops, SparseCore 0:
  32.2 72.2 all-reduce.1
